TPU v7x, 512 devices: a whole 4x8x8 slice. The times are simulated.
512 devices in a mesh: seq: 256 (over y, z, x), head: 2 (over core).
Axes of the slice: x: 4, y: 8, z: 8, core: 2. Of those that a mesh axis runs over, the one named last changes fastest.
Arguments:
- hidden: bfloat16 [32768, 1024], P('seq'), may hold values from -24 to 24
- query_weight: bfloat16 [1024, 512], P(None, 'head'), may hold values from -0.1875 to 0.1875
- key_weight: bfloat16 [1024, 512], P(None, 'head'), may hold values from -0.1875 to 0.1875
- values: bfloat16 [32768, 512], P('seq', 'head'), may hold values from -6 to 6
- grad_out: bfloat16 [32768, 512], P('seq', 'head'), may hold values from -6 to 6
- random_feats: float32 [8, 64, 256], P('head'), may hold values from -4 to 4
Outputs:
- grad_hidden: float32 [32768, 1024], P('seq')
- grad_values: bfloat16 [32768, 512], P('seq', 'head')
- grad_query_weight: float32 [1024, 512], P('seq', 'head')
- grad_key_weight: float32 [1024, 512], P('seq', 'head')
All inputs are finite; a program needn't handle non-finite values.
Results may differ from a plain program's by a relative error of at most 0.0038.
Values sent between devices are 32-bit elements; how exact they have to be, the bound alone decides.
A program may use at most 64 MiB of HBM per device.

v0:
```python
import jax
import jax.numpy as jnp
from jax import lax
from jax.sharding import Mesh
from jax.sharding import PartitionSpec as P

SEQ = ("seq_0", "seq_1", "seq_2")


HIGH = lax.Precision.HIGHEST


def packed_total(arrays, axis):
    line, at, outs = (jnp.concatenate([a.reshape(-1) for a in arrays]), 0, [])
    total = lax.psum(line, axis)
    for a in arrays:
        outs.append(total[at : at + a.size].reshape(a.shape))
        at += a.size
    return tuple(outs)


def summed_rows(shard, axes, dim):
    if not axes:
        return shard
    nearer = lax.psum_scatter(shard, axes[0], scatter_dimension=dim, tiled=True)
    return summed_rows(nearer, axes[1:], dim)


def features(rows, table, feat_count):
    logits = jnp.einsum("tgd,gdm->gtm", rows, table, precision=HIGH)
    half_norm = 0.5 * jnp.sum(rows * rows, axis=2).T
    return jnp.exp(logits - half_norm[:, :, None]) * feat_count ** (-0.5)


def feature_grad(rows, feats, grads, table, feature_scale, tok_count):
    weighted = feats * grads
    back = jnp.einsum("gtm,gdm->tgd", weighted, table, precision=HIGH)
    totals = jnp.sum(weighted, axis=2).T
    result = (back - rows * totals[:, :, None]) * feature_scale
    return result.reshape(tok_count, -1).astype(jnp.bfloat16)


def back_product(grads, weight):
    return lax.dot_general(
        grads, weight, (((1,), (1,)), ((), ())), preferred_element_type=jnp.float32
    )


def shards(hidden, query_weight, key_weight, values, grad_out, random_feats):
    tok_count = hidden.shape[0]
    group_count = random_feats.shape[0]
    head_dim = random_feats.shape[1]
    feat_count = random_feats.shape[2]
    feature_scale = head_dim ** (-0.25)
    query_proj = jnp.dot(hidden, query_weight, preferred_element_type=jnp.float32)
    key_proj = jnp.dot(hidden, key_weight, preferred_element_type=jnp.float32)
    query_rows = (query_proj * feature_scale).reshape(tok_count, group_count, head_dim)
    key_rows = (key_proj * feature_scale).reshape(tok_count, group_count, head_dim)
    value_rows = values.astype(jnp.float32).reshape(tok_count, group_count, head_dim)
    key_feats = features(key_rows, random_feats, feat_count)
    local_state = jnp.einsum("tgj,gtm->gjm", value_rows, key_feats, precision=HIGH)
    local_normal = jnp.sum(key_feats, axis=1)
    value_state, normalizer = packed_total((local_state, local_normal), SEQ)
    query_feats = features(query_rows, random_feats, feat_count)
    numerator = jnp.einsum("gtm,gjm->tgj", query_feats, value_state, precision=HIGH)
    denominator = jnp.einsum("gtm,gm->tg", query_feats, normalizer, precision=HIGH)
    attended = numerator / denominator[:, :, None]
    upstream = grad_out.astype(jnp.float32).reshape(tok_count, group_count, head_dim)
    grad_numer = upstream / denominator[:, :, None]
    grad_denom = -jnp.sum(upstream * attended, axis=2) / denominator
    grad_qfeat = (
        jnp.einsum("tgj,gjm->gtm", grad_numer, value_state, precision=HIGH)
        + grad_denom.T[:, :, None] * normalizer[:, None, :]
    )
    part_state = jnp.einsum("gtm,tgj->gjm", query_feats, grad_numer, precision=HIGH)
    part_normal = jnp.einsum("gtm,tg->gm", query_feats, grad_denom, precision=HIGH)
    grad_query = feature_grad(
        query_rows, query_feats, grad_qfeat, random_feats, feature_scale, tok_count
    )
    grad_state, grad_normal = packed_total((part_state, part_normal), SEQ)
    grad_kfeat = (
        jnp.einsum("tgj,gjm->gtm", value_rows, grad_state, precision=HIGH) + grad_normal[:, None, :]
    )
    grad_value = jnp.einsum("gtm,gjm->tgj", key_feats, grad_state, precision=HIGH)
    grad_values = grad_value.reshape(tok_count, -1).astype(jnp.bfloat16)
    grad_key = feature_grad(key_rows, key_feats, grad_kfeat, random_feats, feature_scale, tok_count)
    both_parts = back_product(grad_query, query_weight) + back_product(grad_key, key_weight)
    grad_hidden = lax.psum(both_parts, "head")
    full_query = lax.dot_general(
        hidden, grad_query, (((0,), (0,)), ((), ())), preferred_element_type=jnp.float32
    )
    full_key = lax.dot_general(
        hidden, grad_key, (((0,), (0,)), ((), ())), preferred_element_type=jnp.float32
    )
    grad_query_weight, grad_key_weight = (
        summed_rows(full_query, SEQ, 0),
        summed_rows(full_key, SEQ, 0),
    )
    return (grad_hidden, grad_values, grad_query_weight, grad_key_weight)


def solution(mesh):
    torus = Mesh(
        mesh.devices.reshape(8, 8, 4, mesh.shape["head"]), ("seq_0", "seq_1", "seq_2", "head")
    )
    placed = (
        P(SEQ, None),
        P(None, "head"),
        P(None, "head"),
        P(SEQ, "head"),
        P(SEQ, "head"),
        P("head", None, None),
    )
    return jax.shard_map(
        shards,
        mesh=torus,
        in_specs=placed,
        out_specs=(P(SEQ, None), P(SEQ, "head"), P(SEQ, "head"), P(SEQ, "head")),
        check_vma=False,
    )
```

profile of v0, /device:TPU:1, one launch (start us, length us, event | category | flops | bytes accessed | tf_op | source)
XLA Modules:
  0.0 701.9 jit_solution(13962535049503031171)
XLA Ops:
  7.2 1.4 convolution_multiply_fusion
  8.8 0.8 copy-done.1
  9.6 0.7 fusion.17
  10.3 0.1 copy-done.5
  10.5 0.3 fusion.20
  10.9 0.1 copy.50
  11.0 0.7 pad_maximum_fusion
  11.8 0.9 copy-done.2
  12.7 0.2 convolution_multiply_fusion.1
  13.1 0.8 copy-done.4
  14.0 0.7 fusion.6
  14.7 233.5 %all-reduce.7.cloned.1.call-done = f32[66560]{0:T(1024)} async-done(((f32[66560]{0:T(1024)}), f32[66560]{0:T(1024)}) %all-reduce.7.cloned.1.call-update) | async-done | bytes 266256 | tf_op jit(solution)/shard_map/psum | solution.py:15
  248.1 0.7 slice.40
  248.8 0.9 slice-done
  249.8 0.5 fusion.21
  250.4 0.4 fusion.16
  250.8 0.7 fusion.15
  251.5 0.4 fusion.23
  251.9 0.1 copy.52
  252.1 0.7 pad_maximum_fusion.1
  252.9 0.8 fusion.18
  253.6 0.7 fusion.13
  254.3 1.3 convolution_bitcast_fusion.1
  255.7 227.9 %all-reduce.9.cloned.1.call-done = f32[66560]{0:T(1024)} async-done(((f32[66560]{0:T(1024)}), f32[66560]{0:T(1024)}) %all-reduce.9.cloned.1.call-update) | async-done | bytes 266256 | tf_op jit(solution)/shard_map/psum | solution.py:15
  483.6 0.7 slice-done.1
  484.3 0.9 slice-done.2
  485.3 0.5 fusion.19
  485.8 0.7 fusion.14
  486.5 1.3 convolution_bitcast_fusion
  487.9 35.7 %reduce-scatter.11.cloned.1.call-done = f32[128,256]{0,1:T(8,128)} async-done(((f32[1024,256]{0,1:T(8,128)}), f32[128,256]{0,1:T(8,128)}) %reduce-scatter.11.cloned.1.call-update) | async-done | bytes 131088 | tf_op jit(solution)/shard_map/reduce_scatter | solution.py:25
  523.6 1.6 copy.42
  525.3 0.3 fusion.22
  525.6 41.1 %reduce-scatter.13.cloned.1.call-done = f32[128,256]{0,1:T(8,128)} async-done(((f32[1024,256]{0,1:T(8,128)}), f32[128,256]{0,1:T(8,128)}) %reduce-scatter.13.cloned.1.call-update) | async-done | bytes 131088 | tf_op jit(solution)/shard_map/reduce_scatter | solution.py:25
  566.7 1.7 copy.46
  568.4 1.1 convolution_add_fusion
  569.6 1.3 dynamic-slice
  571.5 0.7 convolution_convert_fusion
  572.2 0.7 copy.34
  572.9 35.6 %reduce-scatter.15.cloned.1.call-done = f32[16,256]{1,0:T(8,128)} async-done(((f32[128,256]{1,0:T(8,128)}), f32[16,256]{1,0:T(8,128)}) %reduce-scatter.15.cloned.1.call-update) | async-done | bytes 16400
  608.5 0.8 copy.43
  609.3 40.4 %reduce-scatter.17.cloned.1.call-done = f32[16,256]{1,0:T(8,128)} async-done(((f32[128,256]{1,0:T(8,128)}), f32[16,256]{1,0:T(8,128)}) %reduce-scatter.17.cloned.1.call-update) | async-done | bytes 16400
  649.7 0.8 copy.47
  650.5 16.4 %all-reduce.2 = (f32[16,256]{0,1:T(8,128)S(1)}, f32[16,256]{0,1:T(8,128)S(1)}) all-reduce(f32[16,256]{0,1:T(8,128)S(1)} %copy.43, f32[16,256]{0,1:T(8,128)S(1)} %copy.47), channel_id=4, replica_groups=mesh['seq_0'=8,'seq_1'=8,'seq_2'=4,'head'=2] {'seq_2'}, use_global_device_ids=true, to_apply=%region_11.0.clone | all-reduce | flops 8192 | bytes 65536
  667.0 0.1 constant_dynamic-slice_fusion
  667.1 0.7 copy.35
  667.8 0.7 copy.36
  668.5 24.7 %all-reduce.11.cloned.1.call-done = f32[128,1024]{1,0:T(8,128)} async-done(((f32[128,1024]{1,0:T(8,128)}), f32[128,1024]{1,0:T(8,128)}) %all-reduce.11.cloned.1.call-update) | async-done | bytes 524304 | tf_op jit(solution)/shard_map/psum | solution.py:88
  693.2 1.9 copy.59
  (42 shorter events, 1.1 us)
Async XLA Ops:
  7.2 4.7 copy-start
  7.2 240.9 %all-reduce.7.cloned.1.call-start = ((), (), s32[]{:S(2)}) async-start(), calls=%async_computation.4 | async-start | bytes 532480 | tf_op jit(solution)/shard_map/psum | solution.py:15
  8.6 1.0 copy-start.1
  9.6 0.8 copy-start.5
  11.7 0.9 copy-start.2
  11.8 471.8 %all-reduce.9.cloned.1.call-start = ((), (), s32[]{:S(2)}) async-start(), calls=%async_computation.5 | async-start | bytes 532480 | tf_op jit(solution)/shard_map/psum | solution.py:15
  13.0 0.8 copy-start.4
  248.8 0.9 slice-start
  252.8 270.8 %reduce-scatter.11.cloned.1.call-start = ((), (), s32[]{:S(2)}) async-start(), calls=%async_computation.7 | async-start | bytes 1179648 | tf_op jit(solution)/shard_map/reduce_scatter | solution.py:25
  255.7 311.0 %reduce-scatter.13.cloned.1.call-start = ((), (), s32[]{:S(2)}) async-start(), calls=%async_computation.8 | async-start | bytes 1179648 | tf_op jit(solution)/shard_map/reduce_scatter | solution.py:25
  483.6 0.7 slice-start.1
  484.3 0.9 slice-start.2
  487.8 120.7 %reduce-scatter.15.cloned.1.call-start = ((), (), s32[]{:S(2)}) async-start(), calls=%async_computation.9 | async-start | bytes 147456
  525.3 43.2 %copy-start.3 = (bf16[1024,256]{1,0:T(8,128)(2,1)S(1)}, bf16[1024,256]{1,0:T(8,128)(2,1)}, u32[]{:S(2)}) copy-start(bf16[1024,256]{1,0:T(8,128)(2,1)} %param.8) | copy-start | bytes 1572868
  525.3 124.4 %reduce-scatter.17.cloned.1.call-start = ((), (), s32[]{:S(2)}) async-start(), calls=%async_computation.10 | async-start | bytes 147456
  568.4 124.8 %all-reduce.11.cloned.1.call-start = ((), (), s32[]{:S(2)}) async-start(), calls=%async_computation.6 | async-start | bytes 1048576 | tf_op jit(solution)/shard_map/psum | solution.py:88
Sparse Core Ops, SparseCore 0:
  13.5 234.5 all-reduce.6
  253.7 229.8 all-reduce.8
  486.4 37.1 reduce-scatter.10
  526.3 40.3 reduce-scatter.12
  569.3 39.1 reduce-scatter.14
  611.1 38.5 reduce-scatter.16
  653.2 39.9 all-reduce.10
where the time goes:
time: 703 us; the launch traced here: 702 us
  waiting for transfers between devices  639 us (91%)
  local copies, waits for them, and re-layouts  17 us (2%)
  blocking collectives  16.4 us (2%)
  between operations  15 us (2%)
  matrix products  12.7 us (2%)
    psum x2, waiting for transfers between devices, packed_total(): total = lax.psum(line, axis)  461 us
    reduce_scatter x2, waiting for transfers between devices, summed_rows(): nearer = lax.psum_scatter(shard, axes[0], scatter_dimension=dim, tiled=True)  76.8 us
    unnamed x9, waiting for transfers between devices  76.1 us
    psum x1, waiting for transfers between devices, shards(): grad_hidden = lax.psum(both_parts, 'head')  24.7 us
    unnamed x1, blocking collectives  16.4 us
  transfers between devices with their start and end apart: 7, of which 7 were waited for; matrix products, arithmetic and copies ran while one was open for 2% of the time, Pallas kernels for 0%

commit v1 on v0

v1 whole, which is shorter than its diff:
```python
import functools

import jax
import jax.numpy as jnp
from jax import lax
from jax.experimental import pallas as pl
from jax.experimental.pallas import tpu as pltpu
from jax.sharding import Mesh
from jax.sharding import PartitionSpec as P

F32 = jnp.float32
BF16 = jnp.bfloat16
Y, Z, X, H = "seq_0", "seq_1", "seq_2", "head"
SEQ = (Y, Z, X)
MESH = pl.DeviceIdType.MESH


def dg(a, b, ca, cb):
    return lax.dot_general(a, b, (((ca,), (cb,)), ((), ())), preferred_element_type=F32)


def split(a):
    hi = a.astype(BF16)
    return hi, (a - hi.astype(F32)).astype(BF16)


def dot2(a, b, ca=1, cb=0):
    hi, lo = split(b)
    return dg(a, hi, ca, cb) + dg(a, lo, ca, cb)


def dot3(a, b, ca=1, cb=0):
    ah, al = split(a)
    bh, bl = split(b)
    return dg(ah, bh, ca, cb) + (dg(ah, bl, ca, cb) + dg(al, bh, ca, cb))


class Exchange:
    def __init__(self, axis, count, recv, sems):
        self.axis, self.count, self.recv, self.sems = axis, count, recv, sems
        self.me = lax.axis_index(axis)

    def start(self, source, target=None):
        for d in range(1, self.count):
            other = lax.rem(self.me + d, self.count)
            pltpu.make_async_remote_copy(
                src_ref=source(other),
                dst_ref=self.recv.at[d - 1] if target is None else target,
                send_sem=self.sems.at[0],
                recv_sem=self.sems.at[1],
                device_id={self.axis: other},
                device_id_type=MESH,
            ).start()

    def wait(self):
        pltpu.make_async_copy(self.recv, self.recv, self.sems.at[1]).wait()

    def drain(self):
        pltpu.make_async_copy(self.recv, self.recv, self.sems.at[0]).wait()

    def total(self, own):
        for d in range(1, self.count):
            own = own + self.recv[d - 1]
        return own


class StateSum:
    def __init__(self, first, last, n, nx, state, r1, p1, r2, p2, r3, full, sems):
        self.state, self.p1, self.p2, self.full = state, p1, p2, full
        self.near = p1.shape[0]
        self.tile = p2.shape[0]
        self.steps = [
            Exchange(first, n, r1, sems.at[0]),
            Exchange(X, nx, r2, sems.at[1]),
            Exchange(last, n, r3, sems.at[2]),
            Exchange(X, nx, r2, sems.at[3]),
            Exchange(first, n, r1, sems.at[4]),
        ]
        self.base = pl.multiple_of(lax.axis_index(first) * self.near, self.near)
        self.x = lax.axis_index(X)

    def rows(self, start, count):
        return pl.ds(pl.multiple_of(start, 8), count)

    def start(self):
        self.steps[0].start(lambda j: self.state.at[self.rows(j * self.near, self.near)])

    def second(self):
        self.steps[0].wait()
        self.p1[...] = self.steps[0].total(self.state[self.rows(self.base, self.near)])
        self.steps[1].start(lambda j: self.p1.at[self.rows(j * self.tile, self.tile)])

    def third(self):
        self.steps[1].wait()
        self.p2[...] = self.steps[1].total(self.p1[self.rows(self.x * self.tile, self.tile)])
        self.steps[2].start(lambda j: self.p2)

    def fourth(self):
        self.steps[2].wait()
        spot = self.rows(self.base + self.x * self.tile, self.tile)
        self.full[spot] = self.steps[2].total(self.p2[...])
        self.steps[3].start(lambda j: self.full.at[spot], self.full.at[spot])

    def fifth(self):
        self.steps[3].wait()
        spot = self.rows(self.base, self.near)
        self.steps[4].start(lambda j: self.full.at[spot], self.full.at[spot])

    def finish(self):
        self.steps[4].wait()

    def drain(self):
        for step in self.steps:
            step.drain()


class RowSum:
    def __init__(self, order, counts, source, recvs, total, sems):
        self.source, self.result = source, total
        self.steps = [
            Exchange(axis, counts[axis], recvs[axis], sems.at[i]) for i, axis in enumerate(order)
        ]

    def start(self):
        self.steps[0].start(lambda j: self.source.at[0])

    def move(self, i):
        self.steps[i].wait()
        total = self.steps[i].total(self.source[i])
        if i == 2:
            self.result[...] = total
        else:
            self.source[i + 1] = total
            self.steps[i + 1].start(lambda j: self.source.at[i + 1])

    def drain(self):
        for step in self.steps:
            step.drain()


class WeightSum:
    def __init__(self, counts, tiles, rx, t1, ry, t2, rz, sems):
        self.tiles, self.t1, self.t2 = tiles, t1, t2
        self.x = Exchange(X, counts[X], rx, sems.at[0])
        self.y = Exchange(Y, counts[Y], ry, sems.at[1])
        self.z = Exchange(Z, counts[Z], rz, sems.at[2])

    def start(self):
        self.x.start(lambda j: self.tiles.at[j])

    def second(self):
        self.x.wait()
        self.t1[...] = self.x.total(self.tiles[self.x.me]).reshape(self.t1.shape)
        self.y.start(lambda j: self.t1.at[j])

    def third(self):
        self.y.wait()
        self.t2[...] = self.y.total(self.t1[self.y.me])
        self.z.start(lambda j: self.t2.at[j])

    def finish(self, out):
        self.z.wait()
        tile = self.z.total(self.t2[self.z.me])
        half = out.shape[0]
        out[:, 0:128] = tile[0:half]
        out[:, 128:256] = tile[half : 2 * half]

    def drain(self):
        for step in (self.x, self.y, self.z):
            step.drain()


def to_tiles(product, tiles):
    pairs = tiles.shape[0] // 2
    shape = (tiles.shape[1], pairs, 8, 128)
    left = product[:, 0:128].reshape(shape)
    right = product[:, 128:256].reshape(shape)
    upper = lax.broadcasted_iota(jnp.int32, (tiles.shape[1], 8, 128), 1) < 4
    for p in range(pairs):
        a, b = left[:, p], right[:, p]
        tiles[2 * p] = jnp.where(upper, a, pltpu.roll(b, 4, 1))
        tiles[2 * p + 1] = jnp.where(upper, pltpu.roll(a, 4, 1), b)


def kernel(counts, heads, dh, feat, hid, wq, wk, val, gout, tab, gh, gv, gq, gk, *scratch):
    (qs, ks, fa, fb, st, r1, p1, r2, p2, r3, full, st_sem) = scratch[:12]
    (zsrc, zy, zx, zz, ztot, z_sem) = scratch[12:18]
    (tiles, rx, t1, ry, t2, rz, w_sem) = scratch[18:25]
    (part, rpart, part_sem) = scratch[25:]
    ny, nz, nx = counts[Y], counts[Z], counts[X]
    scale = dh ** (-0.25)
    norm = feat ** (-0.5)

    barrier = pltpu.get_barrier_semaphore()
    partners = 0
    for axis, n in ((Y, ny), (Z, nz), (X, nx), (H, 2)):
        me = lax.axis_index(axis)
        for d in range(1, n):
            pl.semaphore_signal(
                barrier, inc=1, device_id={axis: lax.rem(me + d, n)}, device_id_type=MESH
            )
            partners += 1

    def state_sum(c):
        return [
            StateSum(
                (Y, Z)[i], (Z, Y)[i], ny, nx, st.at[c, i], r1.at[c, i], p1.at[c, i], r2.at[c, i],
                p2.at[c, i], r3.at[c, i], full.at[c, i], st_sem.at[c, i],
            )
            for i in range(2)
        ]

    def row_sum(c, order):
        recvs = {Y: zy.at[c], X: zx.at[c], Z: zz.at[c]}
        return RowSum(order, counts, zsrc.at[c], recvs, ztot.at[c], z_sem.at[c])

    def weight_sum(c):
        return WeightSum(
            counts, tiles.at[c], rx.at[c], t1.at[c], ry.at[c], t2.at[c], rz.at[c], w_sem.at[c]
        )

    usum, gsum = state_sum(0), state_sum(1)
    zsum, gzsum = row_sum(0, (Y, X, Z)), row_sum(1, (X, Y, Z))
    qsum, ksum = weight_sum(0), weight_sum(1)

    def cols(h):
        return slice(h * dh, (h + 1) * dh)

    def wide(h):
        return slice(h * feat, (h + 1) * feat)

    def features(rows, h):
        own = rows[:, cols(h)]
        logits = dot3(own, tab[h])
        half = 0.5 * jnp.sum(own * own, axis=1, keepdims=True)
        return jnp.exp(logits - half) * norm

    def put_state(c, h, block):
        st[c, 0, cols(h)] = block[:, 0:128]
        st[c, 1, cols(h)] = block[:, 128:256]

    def state(c, h):
        return jnp.concatenate([full[c, 0, cols(h)], full[c, 1, cols(h)]], axis=1)

    k = dg(hid[...], wk[...], 1, 0) * scale
    ks[...] = k
    vt = val[...].astype(F32).T.astype(BF16)
    for h in range(heads):
        b = features(k, h)
        fb[:, wide(h)] = b
        zsrc[0, 0, :, wide(h)] = jnp.sum(b, axis=0, keepdims=True)
        put_state(0, h, dot2(vt[cols(h)], b))
    pl.semaphore_wait(barrier, partners)
    zsum.start()
    for s in usum:
        s.start()

    q = dg(hid[...], wq[...], 1, 0) * scale
    qs[...] = q
    for h in range(heads):
        fa[:, wide(h)] = features(q, h)
    hid_t = hid[...].astype(F32).T.astype(BF16)
    zsum.move(0)
    for s in usum:
        s.second()
    zsum.move(1)
    for s in usum:
        s.third()
    zsum.move(2)

    g = gout[...].astype(F32)
    inv, gn = [], []
    for h in range(heads):
        a = fa[:, wide(h)]
        den = jnp.sum(a * ztot[0, :, wide(h)], axis=1, keepdims=True)
        inv.append(1.0 / den)
        gn.append(g[:, cols(h)] / den)
    gnt = jnp.concatenate(gn, axis=1).T
    for h in range(heads):
        put_state(1, h, dot3(gnt[cols(h)], fa[:, wide(h)]))
    for s in gsum:
        s.start()
    for s in usum:
        s.fourth()
    for s in usum:
        s.fifth()
    for s in gsum:
        s.second()
    for s in gsum:
        s.third()
    for s in usum:
        s.finish()

    gd = []
    for h in range(heads):
        a = fa[:, wide(h)]
        o = dot3(a, state(0, h), 1, 1) * inv[h]
        gd.append(-jnp.sum(g[:, cols(h)] * o, axis=1, keepdims=True) * inv[h])
        zsrc[1, 0, :, wide(h)] = jnp.sum(gd[h] * a, axis=0, keepdims=True)
    gzsum.start()
    for s in gsum:
        s.fourth()

    def back(rows, h, weighted):
        got = dot3(weighted, tab[h], 1, 1)
        total = jnp.sum(weighted, axis=1, keepdims=True)
        return ((got - rows[:, cols(h)] * total) * scale).astype(BF16)

    dq = []
    for h in range(heads):
        ga = dot3(gn[h], state(0, h)) + gd[h] * ztot[0, :, wide(h)]
        dq.append(back(qs, h, fa[:, wide(h)] * ga))
    dq = jnp.concatenate(dq, axis=1)
    gzsum.move(0)
    for s in gsum:
        s.fifth()
    to_tiles(dg(hid_t, dq, 1, 0), tiles.at[0])
    qsum.start()
    part[...] = dg(dq, wq[...], 1, 1)
    gzsum.move(1)
    for s in gsum:
        s.finish()
    for h in range(heads):
        gv[:, cols(h)] = dot3(fb[:, wide(h)], state(1, h), 1, 1).astype(BF16)
    gzsum.move(2)

    dk = []
    for h in range(heads):
        gb = dot2(val[:, cols(h)], state(1, h)) + ztot[1, :, wide(h)]
        dk.append(back(ks, h, fb[:, wide(h)] * gb))
    dk = jnp.concatenate(dk, axis=1)
    to_tiles(dg(hid_t, dk, 1, 0), tiles.at[1])
    ksum.start()
    part[...] += dg(dk, wk[...], 1, 1)
    swap = pltpu.make_async_remote_copy(
        src_ref=part,
        dst_ref=rpart,
        send_sem=part_sem.at[0],
        recv_sem=part_sem.at[1],
        device_id={H: 1 - lax.axis_index(H)},
        device_id_type=MESH,
    )
    swap.start()
    qsum.second()
    qsum.third()
    swap.wait_recv()
    gh[...] = part[...] + rpart[...]
    qsum.finish(gq)
    ksum.second()
    ksum.third()
    ksum.finish(gk)
    swap.wait_send()
    for s in usum + gsum + [zsum, gzsum, qsum, ksum]:
        s.drain()


def shards(counts, hidden, query_weight, key_weight, values, grad_out, random_feats):
    toks, depth = hidden.shape
    heads, dh, feat = random_feats.shape
    width = heads * dh
    ny, nz, nx = counts[Y], counts[Z], counts[X]
    near = width // ny
    tile = near // nx
    own_rows = depth // (ny * nz * nx)
    row = heads * feat
    vm = lambda *shape: pltpu.VMEM(shape, F32)
    dma = lambda *shape: pltpu.SemaphoreType.DMA(shape)
    scratch = [
        vm(toks, width),
        vm(toks, width),
        vm(toks, row),
        vm(toks, row),
        vm(2, 2, width, 128),
        vm(2, 2, ny - 1, near, 128),
        vm(2, 2, near, 128),
        vm(2, 2, nx - 1, tile, 128),
        vm(2, 2, tile, 128),
        vm(2, 2, nz - 1, tile, 128),
        vm(2, 2, width, 128),
        dma(2, 2, 5, 2),
        vm(2, 3, 1, row),
        vm(2, ny - 1, 1, row),
        vm(2, nx - 1, 1, row),
        vm(2, nz - 1, 1, row),
        vm(2, 1, row),
        dma(2, 3, 2),
        vm(2, nx, ny * nz, 8, 128),
        vm(2, nx - 1, ny * nz, 8, 128),
        vm(2, ny, nz, 8, 128),
        vm(2, ny - 1, nz, 8, 128),
        vm(2, nz, 8, 128),
        vm(2, nz - 1, 8, 128),
        dma(2, 3, 2),
        vm(toks, depth),
        vm(toks, depth),
        dma(2),
    ]
    return pl.pallas_call(
        functools.partial(kernel, counts, heads, dh, feat),
        out_shape=(
            jax.ShapeDtypeStruct((toks, depth), F32),
            jax.ShapeDtypeStruct((toks, width), BF16),
            jax.ShapeDtypeStruct((own_rows, width), F32),
            jax.ShapeDtypeStruct((own_rows, width), F32),
        ),
        in_specs=[pl.BlockSpec(memory_space=pltpu.VMEM)] * 6,
        out_specs=(pl.BlockSpec(memory_space=pltpu.VMEM),) * 4,
        scratch_shapes=scratch,
        compiler_params=pltpu.CompilerParams(collective_id=0, has_side_effects=True),
        name="favor_backward",
    )(hidden, query_weight, key_weight, values, grad_out, random_feats)


def build(torus):
    counts = {axis: torus.shape[axis] for axis in SEQ}
    return jax.shard_map(
        functools.partial(shards, counts),
        mesh=torus,
        in_specs=(
            P(SEQ, None),
            P(None, H),
            P(None, H),
            P(SEQ, H),
            P(SEQ, H),
            P(H, None, None),
        ),
        out_specs=(P(SEQ, None), P(SEQ, H), P(SEQ, H), P(SEQ, H)),
        check_vma=False,
    )


def solution(mesh):
    devices = mesh.devices.reshape(8, 8, 4, mesh.shape["head"])
    return build(Mesh(devices, (Y, Z, X, H)))
```

time: 703 us -> 94.1 us (0.13)
  the two profiles are of different devices: /device:TPU:1 before, /device:TPU:4 now
where the time goes in v1:
time: 94.1 us; the launch traced here: 93.8 us
  Pallas kernels  89.3 us (95%)
  local copies, waits for them, and re-layouts  3.86 us (4%)
    pallas_call x1, Pallas kernels, shards(): pl.pallas_call(functools.partial(kernel, counts, heads, dh, feat), out_sh...  89.3 us
    unnamed x10, local copies, waits for them, and re-layouts  3.86 us

profile of v1, /device:TPU:4, one launch (start us, length us, event | category | flops | bytes accessed | tf_op | source)
XLA Modules:
  0.0 93.8 jit_solution(4082533719153675432)
XLA Ops:
  0.6 89.3 %favor_backward.1 = (f32[128,1024]{1,0:T(8,128)}, bf16[128,256]{1,0:T(8,128)(2,1)}, f32[4,256]{1,0:T(4,128)}, f32[4,256]{1,0:T(4,128)}) custom-call(bf16[128,1024]{1,0:T(8,128)(2,1)} %hid.1, bf16[1024,256]{1,0:T(8,128)(2,1)} %wq.1, bf16[1024,256]{1,0:T(8,128)(2,1)} %wk.1, bf16[128,256]{1,0:T(8,128)(2,1)} %val.1, bf16[128,256]{1,0:T(8,128)(2,1)} %gout.1, ...), custom_call_target="tpu_custom_call" | custom-call | tf_op jit(solution)/shard_map/favor_backward/pallas_call | solution.py:398
  90.0 0.0 copy-start
  90.0 1.9 %copy.14 = f32[128,1024]{1,0:T(8,128)} copy(f32[128,1024]{1,0:T(8,128)} %get-tuple-element.8) | data formatting | bytes 1048576
  91.9 0.0 copy-done
  91.9 0.0 copy-start.2
  91.9 0.6 copy.15
  92.5 0.0 copy-done.2
  92.5 0.0 copy-start.1
  92.6 0.6 copy.16
  93.1 0.1 copy-done.1
  93.2 0.6 copy.17
Async XLA Ops:
  90.0 1.9 %copy-start = (bf16[128,256]{1,0:T(8,128)(2,1)S(1)}, bf16[128,256]{1,0:T(8,128)(2,1)}, u32[]{:S(2)}) copy-start(bf16[128,256]{1,0:T(8,128)(2,1)} %get-tuple-element.9) | copy-start | bytes 196612
  91.9 0.7 copy-start.2
  92.5 0.7 copy-start.1

commit v2 on v1

--- a/solution.py
+++ b/solution.py
@@ -139,54 +139,91 @@
 
 
 class WeightSum:
-    def __init__(self, counts, tiles, rx, t1, ry, t2, rz, sems):
-        self.tiles, self.t1, self.t2 = tiles, t1, t2
+    def __init__(self, counts, hid_t, grads, rx, part, r1, p1, r2, sems):
+        self.hid_t, self.grads, self.part, self.p1 = hid_t, grads, part, p1
         self.x = Exchange(X, counts[X], rx, sems.at[0])
-        self.y = Exchange(Y, counts[Y], ry, sems.at[1])
-        self.z = Exchange(Z, counts[Z], rz, sems.at[2])
+        self.near = p1.shape[1]
+        self.one = [
+            Exchange(axis, counts[axis], r1.at[i], sems.at[1 + i]) for i, axis in enumerate((Y, Z))
+        ]
+        self.two = [
+            Exchange(axis, counts[axis], r2.at[i], sems.at[3 + i]) for i, axis in enumerate((Z, Y))
+        ]
 
     def start(self):
-        self.x.start(lambda j: self.tiles.at[j])
+        self.x.start(lambda j: self.grads)
 
     def second(self):
         self.x.wait()
-        self.t1[...] = self.x.total(self.tiles[self.x.me]).reshape(self.t1.shape)
-        self.y.start(lambda j: self.t1.at[j])
+        for i in range(2):
+            side = slice(i * 128, (i + 1) * 128)
+            total = None
+            for s in range(self.x.count):
+                rows = self.grads[:, side] if s == 0 else self.x.recv[s - 1, :, side]
+                term = dg(self.hid_t[i, s], rows.astype(BF16), 1, 0)
+                total = term if total is None else total + term
+            self.part[i] = total
+            self.one[i].start(
+                lambda j, i=i: self.part.at[i, pl.ds(pl.multiple_of(j * self.near, 8), self.near)]
+            )
 
     def third(self):
-        self.y.wait()
-        self.t2[...] = self.y.total(self.t1[self.y.me])
-        self.z.start(lambda j: self.t2.at[j])
+        for i in range(2):
+            one = self.one[i]
+            one.wait()
+            own = self.part[i, pl.ds(pl.multiple_of(one.me * self.near, 8), self.near)]
+            self.p1[i] = one.total(own)
+            self.two[i].start(
+                lambda j, i=i: self.p1.at[i, pl.ds(pl.multiple_of(lax.div(j, 2) * 8, 8), 8)]
+            )
 
     def finish(self, out):
-        self.z.wait()
-        tile = self.z.total(self.t2[self.z.me])
-        half = out.shape[0]
-        out[:, 0:128] = tile[0:half]
-        out[:, 128:256] = tile[half : 2 * half]
+        for i in range(2):
+            two = self.two[i]
+            two.wait()
+            tile = two.total(self.p1[i, pl.ds(pl.multiple_of(lax.div(two.me, 2) * 8, 8), 8)])
+            low = lax.rem(two.me, 2) == 0
+            out[:, i * 128 : (i + 1) * 128] = jnp.where(low, tile[0:4], tile[4:8])
 
     def drain(self):
-        for step in (self.x, self.y, self.z):
+        for step in [self.x] + self.one + self.two:
             step.drain()
 
 
-def to_tiles(product, tiles):
-    pairs = tiles.shape[0] // 2
-    shape = (tiles.shape[1], pairs, 8, 128)
-    left = product[:, 0:128].reshape(shape)
-    right = product[:, 128:256].reshape(shape)
-    upper = lax.broadcasted_iota(jnp.int32, (tiles.shape[1], 8, 128), 1) < 4
-    for p in range(pairs):
-        a, b = left[:, p], right[:, p]
-        tiles[2 * p] = jnp.where(upper, a, pltpu.roll(b, 4, 1))
-        tiles[2 * p + 1] = jnp.where(upper, pltpu.roll(a, 4, 1), b)
+def interleave(upper, a, b):
+    return jnp.where(upper, a, pltpu.roll(b, 4, 1)), jnp.where(upper, pltpu.roll(a, 4, 1), b)
+
+
+def halves(shape):
+    return lax.broadcasted_iota(jnp.int32, shape, 1) < 4
+
+
+def by_x(turned, out):
+    nx, rows, toks = out.shape
+    tiles = turned.reshape(rows // 8, 2, nx // 2, 8, toks)
+    upper = halves((rows // 8, 8, toks))
+    for p in range(nx // 2):
+        even, odd = interleave(upper, tiles[:, 0, p], tiles[:, 1, p])
+        out[2 * p] = even.reshape(rows, toks)
+        out[2 * p + 1] = odd.reshape(rows, toks)
+
+
+def swapped(block, ny, nz):
+    rows, toks = block.shape
+    tiles = block.reshape(ny // 2, 2, nz // 2, 8, toks)
+    upper = halves((ny // 2, 8, toks))
+    out = []
+    for w in range(nz // 2):
+        out.extend(interleave(upper, tiles[:, 0, w], tiles[:, 1, w]))
+    return jnp.concatenate([t.reshape(ny * 4, toks) for t in out], axis=0)
 
 
 def kernel(counts, heads, dh, feat, hid, wq, wk, val, gout, tab, gh, gv, gq, gk, *scratch):
     (qs, ks, fa, fb, st, r1, p1, r2, p2, r3, full, st_sem) = scratch[:12]
     (zsrc, zy, zx, zz, ztot, z_sem) = scratch[12:18]
-    (tiles, rx, t1, ry, t2, rz, w_sem) = scratch[18:25]
-    (part, rpart, part_sem) = scratch[25:]
+    (grads, rx, wpart, w1, wp1, w2, w_sem) = scratch[18:25]
+    (turned, rturned, hid_t, turned_sem) = scratch[25:29]
+    (part, rpart, part_sem) = scratch[29:]
     ny, nz, nx = counts[Y], counts[Z], counts[X]
     scale = dh ** (-0.25)
     norm = feat ** (-0.5)
@@ -216,12 +253,13 @@
 
     def weight_sum(c):
         return WeightSum(
-            counts, tiles.at[c], rx.at[c], t1.at[c], ry.at[c], t2.at[c], rz.at[c], w_sem.at[c]
+            counts, hid_t, grads.at[c], rx.at[c], wpart.at[c], w1.at[c], wp1.at[c], w2.at[c], w_sem.at[c]
         )
 
     usum, gsum = state_sum(0), state_sum(1)
-    zsum, gzsum = row_sum(0, (Y, X, Z)), row_sum(1, (X, Y, Z))
+    zsum, gzsum = row_sum(0, (X, Y, Z)), row_sum(1, (X, Y, Z))
     qsum, ksum = weight_sum(0), weight_sum(1)
+    hsum = Exchange(X, nx, rturned, turned_sem)
 
     def cols(h):
         return slice(h * dh, (h + 1) * dh)
@@ -254,12 +292,13 @@
     zsum.start()
     for s in usum:
         s.start()
+    by_x(hid[...].astype(F32).T, turned)
+    hsum.start(lambda j: turned.at[j])
 
     q = dg(hid[...], wq[...], 1, 0) * scale
     qs[...] = q
     for h in range(heads):
         fa[:, wide(h)] = features(q, h)
-    hid_t = hid[...].astype(F32).T.astype(BF16)
     zsum.move(0)
     for s in usum:
         s.second()
@@ -284,6 +323,11 @@
         s.fourth()
     for s in usum:
         s.fifth()
+    hsum.wait()
+    for i in range(nx):
+        block = turned[hsum.me] if i == 0 else rturned[i - 1]
+        hid_t[0, i] = block.astype(BF16)
+        hid_t[1, i] = swapped(block, ny, nz).astype(BF16)
     for s in gsum:
         s.second()
     for s in gsum:
@@ -314,12 +358,13 @@
     gzsum.move(0)
     for s in gsum:
         s.fifth()
-    to_tiles(dg(hid_t, dq, 1, 0), tiles.at[0])
+    grads[0] = dq.astype(F32)
     qsum.start()
     part[...] = dg(dq, wq[...], 1, 1)
     gzsum.move(1)
     for s in gsum:
         s.finish()
+    qsum.second()
     for h in range(heads):
         gv[:, cols(h)] = dot3(fb[:, wide(h)], state(1, h), 1, 1).astype(BF16)
     gzsum.move(2)
@@ -329,7 +374,7 @@
         gb = dot2(val[:, cols(h)], state(1, h)) + ztot[1, :, wide(h)]
         dk.append(back(ks, h, fb[:, wide(h)] * gb))
     dk = jnp.concatenate(dk, axis=1)
-    to_tiles(dg(hid_t, dk, 1, 0), tiles.at[1])
+    grads[1] = dk.astype(F32)
     ksum.start()
     part[...] += dg(dk, wk[...], 1, 1)
     swap = pltpu.make_async_remote_copy(
@@ -341,17 +386,21 @@
         device_id_type=MESH,
     )
     swap.start()
-    qsum.second()
     qsum.third()
+    ksum.second()
     swap.wait_recv()
     gh[...] = part[...] + rpart[...]
     qsum.finish(gq)
-    ksum.second()
     ksum.third()
     ksum.finish(gk)
     swap.wait_send()
-    for s in usum + gsum + [zsum, gzsum, qsum, ksum]:
+    for s in usum + gsum + [zsum, gzsum, qsum, ksum, hsum]:
         s.drain()
+
+
+def settle(*refs):
+    for source, target in zip(refs[:4], refs[4:]):
+        target[...] = source[...]
 
 
 def shards(counts, hidden, query_weight, key_weight, values, grad_out, random_feats):
@@ -363,6 +412,7 @@
     tile = near // nx
     own_rows = depth // (ny * nz * nx)
     row = heads * feat
+    rows = depth // nx
     vm = lambda *shape: pltpu.VMEM(shape, F32)
     dma = lambda *shape: pltpu.SemaphoreType.DMA(shape)
     scratch = [
@@ -384,31 +434,40 @@
         vm(2, nz - 1, 1, row),
         vm(2, 1, row),
         dma(2, 3, 2),
-        vm(2, nx, ny * nz, 8, 128),
-        vm(2, nx - 1, ny * nz, 8, 128),
-        vm(2, ny, nz, 8, 128),
-        vm(2, ny - 1, nz, 8, 128),
-        vm(2, nz, 8, 128),
-        vm(2, nz - 1, 8, 128),
-        dma(2, 3, 2),
+        vm(2, toks, width),
+        vm(2, nx - 1, toks, width),
+        vm(2, 2, rows, 128),
+        vm(2, 2, ny - 1, rows // ny, 128),
+        vm(2, 2, rows // ny, 128),
+        vm(2, 2, nz - 1, 8, 128),
+        dma(2, 5, 2),
+        vm(nx, rows, toks),
+        vm(nx - 1, rows, toks),
+        pltpu.VMEM((2, nx, rows, toks), BF16),
+        dma(2),
         vm(toks, depth),
         vm(toks, depth),
         dma(2),
     ]
-    return pl.pallas_call(
+    shapes = (
+        jax.ShapeDtypeStruct((toks, depth), F32),
+        jax.ShapeDtypeStruct((toks, width), BF16),
+        jax.ShapeDtypeStruct((own_rows, width), F32),
+        jax.ShapeDtypeStruct((own_rows, width), F32),
+    )
+    vmem = pl.BlockSpec(memory_space=pltpu.VMEM)
+    results = pl.pallas_call(
         functools.partial(kernel, counts, heads, dh, feat),
-        out_shape=(
-            jax.ShapeDtypeStruct((toks, depth), F32),
-            jax.ShapeDtypeStruct((toks, width), BF16),
-            jax.ShapeDtypeStruct((own_rows, width), F32),
-            jax.ShapeDtypeStruct((own_rows, width), F32),
-        ),
-        in_specs=[pl.BlockSpec(memory_space=pltpu.VMEM)] * 6,
-        out_specs=(pl.BlockSpec(memory_space=pltpu.VMEM),) * 4,
+        out_shape=shapes,
+        in_specs=[vmem] * 6,
+        out_specs=(vmem,) * 4,
         scratch_shapes=scratch,
         compiler_params=pltpu.CompilerParams(collective_id=0, has_side_effects=True),
         name="favor_backward",
     )(hidden, query_weight, key_weight, values, grad_out, random_feats)
+    return pl.pallas_call(
+        settle, out_shape=shapes, in_specs=[vmem] * 4, out_specs=(vmem,) * 4, name="settle"
+    )(*results)
 
 
 def build(torus):

time: 94.1 us -> 78.9 us (0.84)
  Pallas kernels: 89.3 us -> 78.1 us
  local copies, waits for them, and re-layouts: 3.86 us -> 0 us
    pallas_call x1, Pallas kernels: 89.3 us -> 76.2 us  [shards(): pl.pallas_call(functools.partial(kernel, counts, heads, dh, feat), out_sh...]
    unnamed x10 -> x0, local copies, waits for them, and re-layouts: 3.86 us -> none
    pallas_call x0 -> x1, Pallas kernels: none -> 1.92 us  [shards(): pl.pallas_call(settle, out_shape=shapes, in_specs=[vmem] * 4, out_specs=(...]
where the time goes in v2:
time: 78.9 us; the launch traced here: 78.7 us
  Pallas kernels  78.1 us (99%)
    pallas_call x1, Pallas kernels, shards(): pl.pallas_call(functools.partial(kernel, counts, heads, dh, feat), out_sh...  76.2 us
    pallas_call x1, Pallas kernels, shards(): pl.pallas_call(settle, out_shape=shapes, in_specs=[vmem] * 4, out_specs=(...  1.92 us

profile of v2, /device:TPU:4, one launch (start us, length us, event | category | flops | bytes accessed | tf_op | source)
XLA Modules:
  0.0 78.7 jit_solution(12255869495678341266)
XLA Ops:
  0.6 76.2 %favor_backward.1 = (f32[128,1024]{1,0:T(8,128)}, bf16[128,256]{1,0:T(8,128)(2,1)}, f32[4,256]{1,0:T(4,128)}, f32[4,256]{1,0:T(4,128)}) custom-call(bf16[128,1024]{1,0:T(8,128)(2,1)} %hid.1, bf16[1024,256]{1,0:T(8,128)(2,1)} %wq.1, bf16[1024,256]{1,0:T(8,128)(2,1)} %wk.1, bf16[128,256]{1,0:T(8,128)(2,1)} %val.1, bf16[128,256]{1,0:T(8,128)(2,1)} %gout.1, ...), custom_call_target="tpu_custom_call" | custom-call | tf_op jit(solution)/shard_map/favor_backward/pallas_call | solution.py:459
  76.8 1.9 %settle.1 = (f32[128,1024]{1,0:T(8,128)}, bf16[128,256]{1,0:T(8,128)(2,1)}, f32[4,256]{1,0:T(4,128)}, f32[4,256]{1,0:T(4,128)}) custom-call(f32[128,1024]{1,0:T(8,128)} %get-tuple-element.8.refs_0_, bf16[128,256]{1,0:T(8,128)(2,1)} %get-tuple-element.9.refs_1_, f32[4,256]{1,0:T(4,128)} %get-tuple-element.10.refs_2_, f32[4,256]{1,0:T(4,128)} %get-tuple-element.11.refs_3_), custom_call_target="tpu_custom_call" | custom-call | tf_op jit(solution)/shard_map/settle/pallas_call | solution.py:468

commit v3 on v2

--- a/solution.py
+++ b/solution.py
@@ -1,4 +1,5 @@
 import functools
+import itertools
 
 import jax
 import jax.numpy as jnp
@@ -36,19 +37,24 @@
 
 
 class Exchange:
-    def __init__(self, axis, count, recv, sems):
-        self.axis, self.count, self.recv, self.sems = axis, count, recv, sems
-        self.me = lax.axis_index(axis)
+    def __init__(self, axes, counts, recv, sems):
+        self.axes, self.recv, self.sems = axes, recv, sems
+        self.counts = [counts[axis] for axis in axes]
+        self.me = [lax.axis_index(axis) for axis in axes]
+        self.moves = other_moves(self.counts)
 
     def start(self, source, target=None):
-        for d in range(1, self.count):
-            other = lax.rem(self.me + d, self.count)
+        places = [
+            [lax.rem(m + d, n) for d in range(n)] for m, n in zip(self.me, self.counts)
+        ]
+        for slot, move in enumerate(self.moves):
+            other = [place[d] for place, d in zip(places, move)]
             pltpu.make_async_remote_copy(
-                src_ref=source(other),
-                dst_ref=self.recv.at[d - 1] if target is None else target,
+                src_ref=source(*other),
+                dst_ref=self.recv.at[slot] if target is None else target,
                 send_sem=self.sems.at[0],
                 recv_sem=self.sems.at[1],
-                device_id={self.axis: other},
+                device_id=dict(zip(self.axes, other)),
                 device_id_type=MESH,
             ).start()
 
@@ -59,95 +65,87 @@
         pltpu.make_async_copy(self.recv, self.recv, self.sems.at[0]).wait()
 
     def total(self, own):
-        for d in range(1, self.count):
-            own = own + self.recv[d - 1]
-        return own
+        parts = [own] + [self.recv[slot] for slot in range(len(self.moves))]
+        while len(parts) > 1:
+            odd = parts[len(parts) // 2 * 2 :]
+            parts = [a + b for a, b in zip(parts[0::2], parts[1::2])] + odd
+        return parts[0]
+
+
+def other_moves(counts):
+    def hops(move):
+        return sum(min(d, n - d) for d, n in zip(move, counts))
+
+    moves = [m for m in itertools.product(*(range(n) for n in counts)) if any(m)]
+    return sorted(moves, key=hops, reverse=True)
 
 
 class StateSum:
-    def __init__(self, first, last, n, nx, state, r1, p1, r2, p2, r3, full, sems):
-        self.state, self.p1, self.p2, self.full = state, p1, p2, full
-        self.near = p1.shape[0]
-        self.tile = p2.shape[0]
-        self.steps = [
-            Exchange(first, n, r1, sems.at[0]),
-            Exchange(X, nx, r2, sems.at[1]),
-            Exchange(last, n, r3, sems.at[2]),
-            Exchange(X, nx, r2, sems.at[3]),
-            Exchange(first, n, r1, sems.at[4]),
-        ]
-        self.base = pl.multiple_of(lax.axis_index(first) * self.near, self.near)
-        self.x = lax.axis_index(X)
-
-    def rows(self, start, count):
-        return pl.ds(pl.multiple_of(start, 8), count)
+    def __init__(self, first, last, counts, state, r1, p1, r2, full, sems):
+        self.state, self.p1, self.full = state, p1, full
+        self.tile, self.nx = p1.shape[0], counts[X]
+        self.scatter = Exchange((first, X), counts, r1, sems.at[0])
+        self.line = Exchange((last,), counts, r2, sems.at[1])
+        self.gather = Exchange((first, X), counts, r1, sems.at[2])
+
+    def spot(self, first, x):
+        return pl.ds(pl.multiple_of((first * self.nx + x) * self.tile, 8), self.tile)
 
     def start(self):
-        self.steps[0].start(lambda j: self.state.at[self.rows(j * self.near, self.near)])
+        self.scatter.start(lambda first, x: self.state.at[self.spot(first, x)])
 
     def second(self):
-        self.steps[0].wait()
-        self.p1[...] = self.steps[0].total(self.state[self.rows(self.base, self.near)])
-        self.steps[1].start(lambda j: self.p1.at[self.rows(j * self.tile, self.tile)])
+        self.scatter.wait()
+        self.p1[...] = self.scatter.total(self.state[self.spot(*self.scatter.me)])
+        self.line.start(lambda j: self.p1)
 
     def third(self):
-        self.steps[1].wait()
-        self.p2[...] = self.steps[1].total(self.p1[self.rows(self.x * self.tile, self.tile)])
-        self.steps[2].start(lambda j: self.p2)
-
-    def fourth(self):
-        self.steps[2].wait()
-        spot = self.rows(self.base + self.x * self.tile, self.tile)
-        self.full[spot] = self.steps[2].total(self.p2[...])
-        self.steps[3].start(lambda j: self.full.at[spot], self.full.at[spot])
-
-    def fifth(self):
-        self.steps[3].wait()
-        spot = self.rows(self.base, self.near)
-        self.steps[4].start(lambda j: self.full.at[spot], self.full.at[spot])
+        self.line.wait()
+        own = self.spot(*self.scatter.me)
+        self.full[own] = self.line.total(self.p1[...])
+        self.gather.start(lambda first, x: self.full.at[own], self.full.at[own])
 
     def finish(self):
-        self.steps[4].wait()
+        self.gather.wait()
 
     def drain(self):
-        for step in self.steps:
+        for step in (self.scatter, self.line, self.gather):
             step.drain()
 
 
 class RowSum:
-    def __init__(self, order, counts, source, recvs, total, sems):
-        self.source, self.result = source, total
-        self.steps = [
-            Exchange(axis, counts[axis], recvs[axis], sems.at[i]) for i, axis in enumerate(order)
-        ]
+    def __init__(self, counts, source, plane, line, result, sems):
+        self.source, self.result = source, result
+        self.plane = Exchange((Y, X), counts, plane, sems.at[0])
+        self.line = Exchange((Z,), counts, line, sems.at[1])
 
     def start(self):
-        self.steps[0].start(lambda j: self.source.at[0])
-
-    def move(self, i):
-        self.steps[i].wait()
-        total = self.steps[i].total(self.source[i])
-        if i == 2:
-            self.result[...] = total
-        else:
-            self.source[i + 1] = total
-            self.steps[i + 1].start(lambda j: self.source.at[i + 1])
+        self.plane.start(lambda *_: self.source.at[0])
+
+    def second(self):
+        self.plane.wait()
+        self.source[1] = self.plane.total(self.source[0])
+        self.line.start(lambda _: self.source.at[1])
+
+    def finish(self):
+        self.line.wait()
+        self.result[...] = self.line.total(self.source[1])
 
     def drain(self):
-        for step in self.steps:
+        for step in (self.plane, self.line):
             step.drain()
 
 
 class WeightSum:
     def __init__(self, counts, hid_t, grads, rx, part, r1, p1, r2, sems):
         self.hid_t, self.grads, self.part, self.p1 = hid_t, grads, part, p1
-        self.x = Exchange(X, counts[X], rx, sems.at[0])
+        self.x = Exchange((X,), counts, rx, sems.at[0])
         self.near = p1.shape[1]
         self.one = [
-            Exchange(axis, counts[axis], r1.at[i], sems.at[1 + i]) for i, axis in enumerate((Y, Z))
+            Exchange((axis,), counts, r1.at[i], sems.at[1 + i]) for i, axis in enumerate((Y, Z))
         ]
         self.two = [
-            Exchange(axis, counts[axis], r2.at[i], sems.at[3 + i]) for i, axis in enumerate((Z, Y))
+            Exchange((axis,), counts, r2.at[i], sems.at[3 + i]) for i, axis in enumerate((Z, Y))
         ]
 
     def start(self):
@@ -158,7 +156,7 @@
         for i in range(2):
             side = slice(i * 128, (i + 1) * 128)
             total = None
-            for s in range(self.x.count):
+            for s in range(self.x.counts[0]):
                 rows = self.grads[:, side] if s == 0 else self.x.recv[s - 1, :, side]
                 term = dg(self.hid_t[i, s], rows.astype(BF16), 1, 0)
                 total = term if total is None else total + term
@@ -171,7 +169,7 @@
         for i in range(2):
             one = self.one[i]
             one.wait()
-            own = self.part[i, pl.ds(pl.multiple_of(one.me * self.near, 8), self.near)]
+            own = self.part[i, pl.ds(pl.multiple_of(one.me[0] * self.near, 8), self.near)]
             self.p1[i] = one.total(own)
             self.two[i].start(
                 lambda j, i=i: self.p1.at[i, pl.ds(pl.multiple_of(lax.div(j, 2) * 8, 8), 8)]
@@ -181,8 +179,8 @@
         for i in range(2):
             two = self.two[i]
             two.wait()
-            tile = two.total(self.p1[i, pl.ds(pl.multiple_of(lax.div(two.me, 2) * 8, 8), 8)])
-            low = lax.rem(two.me, 2) == 0
+            tile = two.total(self.p1[i, pl.ds(pl.multiple_of(lax.div(two.me[0], 2) * 8, 8), 8)])
+            low = lax.rem(two.me[0], 2) == 0
             out[:, i * 128 : (i + 1) * 128] = jnp.where(low, tile[0:4], tile[4:8])
 
     def drain(self):
@@ -219,37 +217,37 @@
 
 
 def kernel(counts, heads, dh, feat, hid, wq, wk, val, gout, tab, gh, gv, gq, gk, *scratch):
-    (qs, ks, fa, fb, st, r1, p1, r2, p2, r3, full, st_sem) = scratch[:12]
-    (zsrc, zy, zx, zz, ztot, z_sem) = scratch[12:18]
-    (grads, rx, wpart, w1, wp1, w2, w_sem) = scratch[18:25]
-    (turned, rturned, hid_t, turned_sem) = scratch[25:29]
-    (part, rpart, part_sem) = scratch[29:]
+    (qs, ks, fa, fb, st, r1, p1, r2, full, st_sem) = scratch[:10]
+    (zsrc, zp, zl, ztot, z_sem) = scratch[10:15]
+    (grads, rx, wpart, w1, wp1, w2, w_sem) = scratch[15:22]
+    (turned, rturned, hid_t, turned_sem) = scratch[22:26]
+    (part, rpart, part_sem) = scratch[26:]
     ny, nz, nx = counts[Y], counts[Z], counts[X]
+    sizes = {**counts, H: 2}
     scale = dh ** (-0.25)
     norm = feat ** (-0.5)
 
     barrier = pltpu.get_barrier_semaphore()
-    partners = 0
-    for axis, n in ((Y, ny), (Z, nz), (X, nx), (H, 2)):
-        me = lax.axis_index(axis)
-        for d in range(1, n):
-            pl.semaphore_signal(
-                barrier, inc=1, device_id={axis: lax.rem(me + d, n)}, device_id_type=MESH
-            )
-            partners += 1
+    partners = set()
+    for axes in ((Y, X), (Z, X), (H,)):
+        for move in other_moves([sizes[axis] for axis in axes]):
+            partners.add(tuple(sorted(zip(axes, move))))
+    partners = sorted({tuple((a, d) for a, d in move if d) for move in partners})
+    for move in partners:
+        place = {a: lax.rem(lax.axis_index(a) + d, sizes[a]) for a, d in move}
+        pl.semaphore_signal(barrier, inc=1, device_id=place, device_id_type=MESH)
 
     def state_sum(c):
         return [
             StateSum(
-                (Y, Z)[i], (Z, Y)[i], ny, nx, st.at[c, i], r1.at[c, i], p1.at[c, i], r2.at[c, i],
-                p2.at[c, i], r3.at[c, i], full.at[c, i], st_sem.at[c, i],
+                (Y, Z)[i], (Z, Y)[i], counts, st.at[c, i], r1.at[c, i], p1.at[c, i], r2.at[c, i],
+                full.at[c, i], st_sem.at[c, i],
             )
             for i in range(2)
         ]
 
-    def row_sum(c, order):
-        recvs = {Y: zy.at[c], X: zx.at[c], Z: zz.at[c]}
-        return RowSum(order, counts, zsrc.at[c], recvs, ztot.at[c], z_sem.at[c])
+    def row_sum(c):
+        return RowSum(counts, zsrc.at[c], zp.at[c], zl.at[c], ztot.at[c], z_sem.at[c])
 
     def weight_sum(c):
         return WeightSum(
@@ -257,9 +255,9 @@
         )
 
     usum, gsum = state_sum(0), state_sum(1)
-    zsum, gzsum = row_sum(0, (X, Y, Z)), row_sum(1, (X, Y, Z))
+    zsum, gzsum = row_sum(0), row_sum(1)
     qsum, ksum = weight_sum(0), weight_sum(1)
-    hsum = Exchange(X, nx, rturned, turned_sem)
+    hsum = Exchange((X,), counts, rturned, turned_sem)
 
     def cols(h):
         return slice(h * dh, (h + 1) * dh)
@@ -288,7 +286,7 @@
         fb[:, wide(h)] = b
         zsrc[0, 0, :, wide(h)] = jnp.sum(b, axis=0, keepdims=True)
         put_state(0, h, dot2(vt[cols(h)], b))
-    pl.semaphore_wait(barrier, partners)
+    pl.semaphore_wait(barrier, len(partners))
     zsum.start()
     for s in usum:
         s.start()
@@ -299,13 +297,10 @@
     qs[...] = q
     for h in range(heads):
         fa[:, wide(h)] = features(q, h)
-    zsum.move(0)
+    zsum.second()
     for s in usum:
         s.second()
-    zsum.move(1)
-    for s in usum:
-        s.third()
-    zsum.move(2)
+    zsum.finish()
 
     g = gout[...].astype(F32)
     inv, gn = [], []
@@ -320,18 +315,14 @@
     for s in gsum:
         s.start()
     for s in usum:
-        s.fourth()
-    for s in usum:
-        s.fifth()
+        s.third()
     hsum.wait()
     for i in range(nx):
-        block = turned[hsum.me] if i == 0 else rturned[i - 1]
+        block = turned[hsum.me[0]] if i == 0 else rturned[i - 1]
         hid_t[0, i] = block.astype(BF16)
         hid_t[1, i] = swapped(block, ny, nz).astype(BF16)
     for s in gsum:
         s.second()
-    for s in gsum:
-        s.third()
     for s in usum:
         s.finish()
 
@@ -343,7 +334,7 @@
         zsrc[1, 0, :, wide(h)] = jnp.sum(gd[h] * a, axis=0, keepdims=True)
     gzsum.start()
     for s in gsum:
-        s.fourth()
+        s.third()
 
     def back(rows, h, weighted):
         got = dot3(weighted, tab[h], 1, 1)
@@ -355,19 +346,15 @@
         ga = dot3(gn[h], state(0, h)) + gd[h] * ztot[0, :, wide(h)]
         dq.append(back(qs, h, fa[:, wide(h)] * ga))
     dq = jnp.concatenate(dq, axis=1)
-    gzsum.move(0)
-    for s in gsum:
-        s.fifth()
+    gzsum.second()
     grads[0] = dq.astype(F32)
     qsum.start()
     part[...] = dg(dq, wq[...], 1, 1)
-    gzsum.move(1)
     for s in gsum:
         s.finish()
-    qsum.second()
     for h in range(heads):
         gv[:, cols(h)] = dot3(fb[:, wide(h)], state(1, h), 1, 1).astype(BF16)
-    gzsum.move(2)
+    gzsum.finish()
 
     dk = []
     for h in range(heads):
@@ -376,6 +363,7 @@
     dk = jnp.concatenate(dk, axis=1)
     grads[1] = dk.astype(F32)
     ksum.start()
+    qsum.second()
     part[...] += dg(dk, wk[...], 1, 1)
     swap = pltpu.make_async_remote_copy(
         src_ref=part,
@@ -408,8 +396,7 @@
     heads, dh, feat = random_feats.shape
     width = heads * dh
     ny, nz, nx = counts[Y], counts[Z], counts[X]
-    near = width // ny
-    tile = near // nx
+    tile = width // (ny * nx)
     own_rows = depth // (ny * nz * nx)
     row = heads * feat
     rows = depth // nx
@@ -421,19 +408,16 @@
         vm(toks, row),
         vm(toks, row),
         vm(2, 2, width, 128),
-        vm(2, 2, ny - 1, near, 128),
-        vm(2, 2, near, 128),
-        vm(2, 2, nx - 1, tile, 128),
+        vm(2, 2, ny * nx - 1, tile, 128),
         vm(2, 2, tile, 128),
         vm(2, 2, nz - 1, tile, 128),
         vm(2, 2, width, 128),
-        dma(2, 2, 5, 2),
-        vm(2, 3, 1, row),
-        vm(2, ny - 1, 1, row),
-        vm(2, nx - 1, 1, row),
+        dma(2, 2, 3, 2),
+        vm(2, 2, 1, row),
+        vm(2, ny * nx - 1, 1, row),
         vm(2, nz - 1, 1, row),
         vm(2, 1, row),
-        dma(2, 3, 2),
+        dma(2, 2, 2),
         vm(2, toks, width),
         vm(2, nx - 1, toks, width),
         vm(2, 2, rows, 128),

time: 78.9 us -> 73.3 us (0.929)
  the two profiles are of different devices: /device:TPU:4 before, /device:TPU:8 now
where the time goes in v3:
time: 73.3 us; the launch traced here: 73.1 us
  Pallas kernels  72.5 us (99%)
    pallas_call x1, Pallas kernels, shards(): pl.pallas_call(functools.partial(kernel, counts, heads, dh, feat), out_sh...  70.6 us
    pallas_call x1, Pallas kernels, shards(): pl.pallas_call(settle, out_shape=shapes, in_specs=[vmem] * 4, out_specs=(...  1.92 us

profile of v3, /device:TPU:8, one launch (start us, length us, event | category | flops | bytes accessed | tf_op | source)
XLA Modules:
  0.0 73.1 jit_solution(13411716182626958836)
XLA Ops:
  0.6 70.6 %favor_backward.1 = (f32[128,1024]{1,0:T(8,128)}, bf16[128,256]{1,0:T(8,128)(2,1)}, f32[4,256]{1,0:T(4,128)}, f32[4,256]{1,0:T(4,128)}) custom-call(bf16[128,1024]{1,0:T(8,128)(2,1)} %hid.1, bf16[1024,256]{1,0:T(8,128)(2,1)} %wq.1, bf16[1024,256]{1,0:T(8,128)(2,1)} %wk.1, bf16[128,256]{1,0:T(8,128)(2,1)} %val.1, bf16[128,256]{1,0:T(8,128)(2,1)} %gout.1, ...), custom_call_target="tpu_custom_call" | custom-call | tf_op jit(solution)/shard_map/favor_backward/pallas_call | solution.py:443
  71.2 1.9 %settle.1 = (f32[128,1024]{1,0:T(8,128)}, bf16[128,256]{1,0:T(8,128)(2,1)}, f32[4,256]{1,0:T(4,128)}, f32[4,256]{1,0:T(4,128)}) custom-call(f32[128,1024]{1,0:T(8,128)} %get-tuple-element.8.refs_0_, bf16[128,256]{1,0:T(8,128)(2,1)} %get-tuple-element.9.refs_1_, f32[4,256]{1,0:T(4,128)} %get-tuple-element.10.refs_2_, f32[4,256]{1,0:T(4,128)} %get-tuple-element.11.refs_3_), custom_call_target="tpu_custom_call" | custom-call | tf_op jit(solution)/shard_map/settle/pallas_call | solution.py:452

commit v4 on v3

--- a/solution.py
+++ b/solution.py
@@ -114,10 +114,10 @@
 
 
 class RowSum:
-    def __init__(self, counts, source, plane, line, result, sems):
+    def __init__(self, first, last, counts, source, plane, line, result, sems):
         self.source, self.result = source, result
-        self.plane = Exchange((Y, X), counts, plane, sems.at[0])
-        self.line = Exchange((Z,), counts, line, sems.at[1])
+        self.plane = Exchange((first, X), counts, plane, sems.at[0])
+        self.line = Exchange((last,), counts, line, sems.at[1])
 
     def start(self):
         self.plane.start(lambda *_: self.source.at[0])
@@ -136,27 +136,75 @@
             step.drain()
 
 
+class TokenRing:
+    def __init__(self, counts, grads, recv, sems):
+        self.grads, self.recv, self.sems = grads, recv, sems
+        self.me, self.count = lax.axis_index(X), counts[X]
+        half = grads.shape[0] // 2
+        self.top, self.low = pl.ds(0, half), pl.ds(half, half)
+
+    def copy(self, i, source, slot, rows, step):
+        return pltpu.make_async_remote_copy(
+            src_ref=source.at[rows],
+            dst_ref=self.recv.at[slot, rows],
+            send_sem=self.sems.at[0, i],
+            recv_sem=self.sems.at[1, i],
+            device_id={X: lax.rem(self.me + step, self.count)},
+            device_id_type=MESH,
+        )
+
+    def copies(self):
+        right, left = 1, self.count - 1
+        return [
+            self.copy(0, self.grads, 1, self.top, right),
+            self.copy(1, self.grads, 2, self.low, left),
+            self.copy(2, self.grads, 1, self.low, right),
+            self.copy(3, self.grads, 2, self.top, left),
+            self.copy(4, self.recv.at[1], 0, self.top, right),
+            self.copy(5, self.recv.at[2], 0, self.low, left),
+        ]
+
+    def start(self):
+        for copy in self.copies()[:4]:
+            copy.start()
+
+    def relay(self):
+        copies = self.copies()
+        for i in range(2):
+            copies[i].wait_recv()
+            copies[4 + i].start()
+
+    def wait(self):
+        for copy in self.copies()[2:]:
+            copy.wait_recv()
+
+    def drain(self):
+        for copy in self.copies():
+            copy.wait_send()
+
+
 class WeightSum:
-    def __init__(self, counts, hid_t, grads, rx, part, r1, p1, r2, sems):
+    def __init__(self, counts, hid_t, grads, rx, ring, part, r1, p1, r2, sems):
         self.hid_t, self.grads, self.part, self.p1 = hid_t, grads, part, p1
-        self.x = Exchange((X,), counts, rx, sems.at[0])
+        self.x = TokenRing(counts, grads, rx, ring)
+        self.count = counts[X]
         self.near = p1.shape[1]
         self.one = [
-            Exchange((axis,), counts, r1.at[i], sems.at[1 + i]) for i, axis in enumerate((Y, Z))
+            Exchange((axis,), counts, r1.at[i], sems.at[i]) for i, axis in enumerate((Y, Z))
         ]
         self.two = [
-            Exchange((axis,), counts, r2.at[i], sems.at[3 + i]) for i, axis in enumerate((Z, Y))
+            Exchange((axis,), counts, r2.at[i], sems.at[2 + i]) for i, axis in enumerate((Z, Y))
         ]
 
     def start(self):
-        self.x.start(lambda j: self.grads)
+        self.x.start()
 
     def second(self):
         self.x.wait()
         for i in range(2):
             side = slice(i * 128, (i + 1) * 128)
             total = None
-            for s in range(self.x.counts[0]):
+            for s in range(self.count):
                 rows = self.grads[:, side] if s == 0 else self.x.recv[s - 1, :, side]
                 term = dg(self.hid_t[i, s], rows.astype(BF16), 1, 0)
                 total = term if total is None else total + term
@@ -216,12 +264,14 @@
     return jnp.concatenate([t.reshape(ny * 4, toks) for t in out], axis=0)
 
 
-def kernel(counts, heads, dh, feat, hid, wq, wk, val, gout, tab, gh, gv, gq, gk, *scratch):
+def kernel(counts, heads, dh, feat, *refs):
+    inputs, (gh, gv, gq, gk), scratch = refs[:6], refs[6:10], refs[10:]
     (qs, ks, fa, fb, st, r1, p1, r2, full, st_sem) = scratch[:10]
     (zsrc, zp, zl, ztot, z_sem) = scratch[10:15]
-    (grads, rx, wpart, w1, wp1, w2, w_sem) = scratch[15:22]
-    (turned, rturned, hid_t, turned_sem) = scratch[22:26]
-    (part, rpart, part_sem) = scratch[26:]
+    (grads, rx, ring_sem, wpart, w1, wp1, w2, w_sem) = scratch[15:23]
+    (turned, rturned, hid_t, turned_sem) = scratch[23:27]
+    (part, rpart, part_sem) = scratch[27:30]
+    hid, wq, wk, val, gout, tab, in_sem = scratch[30:]
     ny, nz, nx = counts[Y], counts[Z], counts[X]
     sizes = {**counts, H: 2}
     scale = dh ** (-0.25)
@@ -237,6 +287,13 @@
         place = {a: lax.rem(lax.axis_index(a) + d, sizes[a]) for a, d in move}
         pl.semaphore_signal(barrier, inc=1, device_id=place, device_id_type=MESH)
 
+    loads = [
+        pltpu.make_async_copy(source, target, in_sem.at[i])
+        for i, (source, target) in enumerate(zip(inputs, (hid, wq, wk, val, gout, tab)))
+    ]
+    for i in (0, 2, 5, 3, 1, 4):
+        loads[i].start()
+
     def state_sum(c):
         return [
             StateSum(
@@ -247,11 +304,17 @@
         ]
 
     def row_sum(c):
-        return RowSum(counts, zsrc.at[c], zp.at[c], zl.at[c], ztot.at[c], z_sem.at[c])
+        return [
+            RowSum(
+                (Y, Z)[i], (Z, Y)[i], counts, zsrc.at[c, i], zp.at[c, i], zl.at[c, i],
+                ztot.at[c, i], z_sem.at[c, i],
+            )
+            for i in range(2)
+        ]
 
     def weight_sum(c):
         return WeightSum(
-            counts, hid_t, grads.at[c], rx.at[c], wpart.at[c], w1.at[c], wp1.at[c], w2.at[c], w_sem.at[c]
+            counts, hid_t, grads.at[c], rx.at[c], ring_sem.at[c], wpart.at[c], w1.at[c], wp1.at[c], w2.at[c], w_sem.at[c]
         )
 
     usum, gsum = state_sum(0), state_sum(1)
@@ -264,6 +327,17 @@
 
     def wide(h):
         return slice(h * feat, (h + 1) * feat)
+
+    def half_row(h):
+        return h // (heads // 2), wide(h % (heads // 2))
+
+    def total_row(c, h):
+        i, spot = half_row(h)
+        return ztot[c, i, :, spot]
+
+    def put_row(c, h, row):
+        i, spot = half_row(h)
+        zsrc[c, i, 0, :, spot] = row
 
     def features(rows, h):
         own = rows[:, cols(h)]
@@ -278,35 +352,44 @@
     def state(c, h):
         return jnp.concatenate([full[c, 0, cols(h)], full[c, 1, cols(h)]], axis=1)
 
+    loads[0].wait()
+    loads[2].wait()
     k = dg(hid[...], wk[...], 1, 0) * scale
     ks[...] = k
+    loads[3].wait()
+    loads[5].wait()
     vt = val[...].astype(F32).T.astype(BF16)
     for h in range(heads):
         b = features(k, h)
         fb[:, wide(h)] = b
-        zsrc[0, 0, :, wide(h)] = jnp.sum(b, axis=0, keepdims=True)
+        put_row(0, h, jnp.sum(b, axis=0, keepdims=True))
         put_state(0, h, dot2(vt[cols(h)], b))
     pl.semaphore_wait(barrier, len(partners))
-    zsum.start()
+    for s in zsum:
+        s.start()
     for s in usum:
         s.start()
     by_x(hid[...].astype(F32).T, turned)
     hsum.start(lambda j: turned.at[j])
 
+    loads[1].wait()
+    loads[4].wait()
     q = dg(hid[...], wq[...], 1, 0) * scale
     qs[...] = q
     for h in range(heads):
         fa[:, wide(h)] = features(q, h)
-    zsum.second()
+    for s in zsum:
+        s.second()
     for s in usum:
         s.second()
-    zsum.finish()
+    for s in zsum:
+        s.finish()
 
     g = gout[...].astype(F32)
     inv, gn = [], []
     for h in range(heads):
         a = fa[:, wide(h)]
-        den = jnp.sum(a * ztot[0, :, wide(h)], axis=1, keepdims=True)
+        den = jnp.sum(a * total_row(0, h), axis=1, keepdims=True)
         inv.append(1.0 / den)
         gn.append(g[:, cols(h)] / den)
     gnt = jnp.concatenate(gn, axis=1).T
@@ -331,8 +414,9 @@
         a = fa[:, wide(h)]
         o = dot3(a, state(0, h), 1, 1) * inv[h]
         gd.append(-jnp.sum(g[:, cols(h)] * o, axis=1, keepdims=True) * inv[h])
-        zsrc[1, 0, :, wide(h)] = jnp.sum(gd[h] * a, axis=0, keepdims=True)
-    gzsum.start()
+        put_row(1, h, jnp.sum(gd[h] * a, axis=0, keepdims=True))
+    for s in gzsum:
+        s.start()
     for s in gsum:
         s.third()
 
@@ -343,27 +427,30 @@
 
     dq = []
     for h in range(heads):
-        ga = dot3(gn[h], state(0, h)) + gd[h] * ztot[0, :, wide(h)]
+        ga = dot3(gn[h], state(0, h)) + gd[h] * total_row(0, h)
         dq.append(back(qs, h, fa[:, wide(h)] * ga))
     dq = jnp.concatenate(dq, axis=1)
-    gzsum.second()
+    for s in gzsum:
+        s.second()
     grads[0] = dq.astype(F32)
     qsum.start()
     part[...] = dg(dq, wq[...], 1, 1)
     for s in gsum:
         s.finish()
+    qsum.x.relay()
+    lifted = [dot2(val[:, cols(h)], state(1, h)) for h in range(heads)]
     for h in range(heads):
         gv[:, cols(h)] = dot3(fb[:, wide(h)], state(1, h), 1, 1).astype(BF16)
-    gzsum.finish()
+    for s in gzsum:
+        s.finish()
 
     dk = []
     for h in range(heads):
-        gb = dot2(val[:, cols(h)], state(1, h)) + ztot[1, :, wide(h)]
+        gb = lifted[h] + total_row(1, h)
         dk.append(back(ks, h, fb[:, wide(h)] * gb))
     dk = jnp.concatenate(dk, axis=1)
     grads[1] = dk.astype(F32)
     ksum.start()
-    qsum.second()
     part[...] += dg(dk, wk[...], 1, 1)
     swap = pltpu.make_async_remote_copy(
         src_ref=part,
@@ -374,25 +461,36 @@
         device_id_type=MESH,
     )
     swap.start()
+    ksum.x.relay()
+    qsum.second()
+    ksum.second()
     qsum.third()
-    ksum.second()
     swap.wait_recv()
     gh[...] = part[...] + rpart[...]
+    ksum.third()
     qsum.finish(gq)
-    ksum.third()
     ksum.finish(gk)
     swap.wait_send()
-    for s in usum + gsum + [zsum, gzsum, qsum, ksum, hsum]:
+    for s in usum + gsum + zsum + gzsum + [qsum, ksum, hsum]:
         s.drain()
 
 
 def settle(*refs):
-    for source, target in zip(refs[:4], refs[4:]):
-        target[...] = source[...]
+    sems = refs[8]
+    copies = [
+        pltpu.make_async_copy(source, target, sems.at[i])
+        for i, (source, target) in enumerate(zip(refs[:4], refs[4:8]))
+    ]
+    for copy in copies:
+        copy.start()
+    for copy in copies:
+        copy.wait()
 
 
 def shards(counts, hidden, query_weight, key_weight, values, grad_out, random_feats):
     toks, depth = hidden.shape
+    inputs = (hidden, query_weight, key_weight, values, grad_out, random_feats)
+    inputs = [pltpu.with_memory_space_constraint(a, pltpu.HBM) for a in inputs]
     heads, dh, feat = random_feats.shape
     width = heads * dh
     ny, nz, nx = counts[Y], counts[Z], counts[X]
@@ -413,18 +511,19 @@
         vm(2, 2, nz - 1, tile, 128),
         vm(2, 2, width, 128),
         dma(2, 2, 3, 2),
-        vm(2, 2, 1, row),
-        vm(2, ny * nx - 1, 1, row),
-        vm(2, nz - 1, 1, row),
-        vm(2, 1, row),
-        dma(2, 2, 2),
+        vm(2, 2, 2, 1, row // 2),
+        vm(2, 2, ny * nx - 1, 1, row // 2),
+        vm(2, 2, nz - 1, 1, row // 2),
+        vm(2, 2, 1, row // 2),
+        dma(2, 2, 2, 2),
         vm(2, toks, width),
         vm(2, nx - 1, toks, width),
+        dma(2, 2, 6),
         vm(2, 2, rows, 128),
         vm(2, 2, ny - 1, rows // ny, 128),
         vm(2, 2, rows // ny, 128),
         vm(2, 2, nz - 1, 8, 128),
-        dma(2, 5, 2),
+        dma(2, 4, 2),
         vm(nx, rows, toks),
         vm(nx - 1, rows, toks),
         pltpu.VMEM((2, nx, rows, toks), BF16),
@@ -432,6 +531,8 @@
         vm(toks, depth),
         vm(toks, depth),
         dma(2),
+        *(pltpu.VMEM(a.shape, a.dtype) for a in inputs),
+        dma(6),
     ]
     shapes = (
         jax.ShapeDtypeStruct((toks, depth), F32),
@@ -443,14 +544,22 @@
     results = pl.pallas_call(
         functools.partial(kernel, counts, heads, dh, feat),
         out_shape=shapes,
-        in_specs=[vmem] * 6,
+        in_specs=[pl.BlockSpec(memory_space=pltpu.HBM)] * 6,
         out_specs=(vmem,) * 4,
         scratch_shapes=scratch,
-        compiler_params=pltpu.CompilerParams(collective_id=0, has_side_effects=True),
+        compiler_params=pltpu.CompilerParams(
+            collective_id=0, has_side_effects=True, vmem_limit_bytes=28 * 2**20
+        ),
         name="favor_backward",
-    )(hidden, query_weight, key_weight, values, grad_out, random_feats)
+    )(*inputs)
     return pl.pallas_call(
-        settle, out_shape=shapes, in_specs=[vmem] * 4, out_specs=(vmem,) * 4, name="settle"
+        settle,
+        out_shape=shapes,
+        in_specs=[vmem] * 4,
+        out_specs=(pl.BlockSpec(memory_space=pl.ANY),) * 4,
+        scratch_shapes=[pltpu.SemaphoreType.DMA((4,))],
+        compiler_params=pltpu.CompilerParams(vmem_limit_bytes=8 * 2**20),
+        name="settle",
     )(*results)
 
 

time: 73.3 us -> 67.5 us (0.921)
  the two profiles are of different devices: /device:TPU:8 before, /device:TPU:2 now
where the time goes in v4:
time: 67.5 us; the launch traced here: 67.4 us
  Pallas kernels  66.7 us (99%)
    pallas_call x1, Pallas kernels, shards(): pl.pallas_call(functools.partial(kernel, counts, heads, dh, feat), out_sh...  65.9 us

profile of v4, /device:TPU:2, one launch (start us, length us, event | category | flops | bytes accessed | tf_op | source)
XLA Modules:
  0.0 67.4 jit_solution(3034827230743686947)
XLA Ops:
  0.6 65.9 %favor_backward.1 = (f32[128,1024]{1,0:T(8,128)S(1)}, bf16[128,256]{1,0:T(8,128)(2,1)S(1)}, f32[4,256]{1,0:T(4,128)S(1)}, f32[4,256]{1,0:T(4,128)S(1)}) custom-call(bf16[128,1024]{1,0:T(8,128)(2,1)} %refs_0_.1, bf16[1024,256]{1,0:T(8,128)(2,1)} %refs_1_.1, bf16[1024,256]{1,0:T(8,128)(2,1)} %refs_2_.1, bf16[128,256]{1,0:T(8,128)(2,1)} %refs_3_.1, ...), custom_call_target="tpu_custom_call" | custom-call | tf_op jit(solution)/shard_map/favor_backward/pallas_call | solution.py:544
  66.5 0.8 %settle.1 = (f32[128,1024]{1,0:T(8,128)}, bf16[128,256]{1,0:T(8,128)(2,1)}, f32[4,256]{1,0:T(4,128)}, f32[4,256]{1,0:T(4,128)}) custom-call(f32[128,1024]{1,0:T(8,128)S(1)} %get-tuple-element.8.refs_0_, bf16[128,256]{1,0:T(8,128)(2,1)S(1)} %get-tuple-element.9.refs_1_, f32[4,256]{1,0:T(4,128)S(1)} %get-tuple-element.10.refs_2_, ...), custom_call_target="tpu_custom_call" | custom-call | tf_op jit(solution)/shard_map/settle/pallas_call | solution.py:555
